TPU v7x, 256 devices: a whole 4x4x8 slice. The times are simulated.
256 devices in a mesh: freq: 8 (over y, x_hi), rec: 32 (over x_lo, z, core).
Axes of the slice: x: 4 (x_hi: 2, x_lo: 2; x = x_hi * 2 + x_lo), y: 4, z: 8, core: 2. Of those that a mesh axis runs over, the one named last changes fastest.
Arguments:
- response: bfloat16 [128, 2, 1792, 1792], P('freq', None, 'rec'), may hold values from -1 to 1, as said below
- direct: float32 [1792, 32, 256], P('rec', 'freq'), may hold values from -6 to 6
- onset: int32 [1792, 32], P('rec', 'freq'), may hold values from 16 to 128
Outputs:
- upgoing: float32 [1792, 32, 256], P('rec', 'freq')
- coda: float32 [1792, 32, 256], P('rec', 'freq')
Inputs may be any that keep to these rules, and one draw needn't show every extreme that they name: response[k, c, r, s] = response[k, c, s, r] for every frequency and part (source-receiver reciprocity).
All inputs are finite; a program needn't handle non-finite values.
Results may differ from a plain program's by a relative error of at most 0.023.
Values may be sent and summed in bfloat16 or wider, within the bound.
A program may use at most 128 MiB of HBM per device.

v0:
```python
import math
import jax
import jax.numpy as jnp
from jax import lax
from jax.sharding import PartitionSpec as P

NF = 128
NT = 256
ITERS = 2


def spectral_tables(length, count):
    samples = jnp.arange(length, dtype=jnp.int32)
    frequency_bins = jnp.arange(1, count + 1, dtype=jnp.int32)
    phase = (samples[:, None] * frequency_bins[None, :] % length).astype(jnp.float32) * (
        2.0 * math.pi / length
    )
    cosine = jnp.cos(phase)
    sine = jnp.sin(phase)
    forward = jnp.stack([cosine, -sine], axis=1)
    inverse = jnp.stack([cosine.T, -sine.T], axis=0) * (2.0 / length)
    return (forward, inverse)


def make_window(onset, length):
    samples = jnp.arange(length, dtype=jnp.int32)
    folded = jnp.minimum(samples, length - samples)
    return (folded[None, None, :] < onset[:, :, None]).astype(jnp.float32)


def to_spectrum(field, forward):
    packed = jnp.einsum("svt,tck->kcvs", field, forward)
    return packed.astype(jnp.bfloat16)


def to_time(spectra, inverse):
    return jnp.einsum("kcvs,ckt->svt", spectra.astype(jnp.float32), inverse)


def complex_apply(block, spectra, conj_sign):
    parts = jnp.einsum("fcrs,fdvs->cdfvr", block, spectra, preferred_element_type=jnp.float32)
    real_out = parts[0, 0] - conj_sign * parts[1, 1]
    imag_out = parts[0, 1] + conj_sign * parts[1, 0]
    return jnp.stack([real_out, imag_out], axis=1)


def body(response, direct, onset):
    forward, inverse = spectral_tables(NT, NF)
    window = make_window(onset, NT)
    coda = jnp.zeros_like(direct)
    upgoing = coda
    for iteration in range(ITERS):
        downgoing = direct + coda
        sources = lax.all_to_all(
            to_spectrum(downgoing, forward), "freq", split_axis=0, concat_axis=2, tiled=True
        )
        gathered = lax.all_gather(sources, "rec", axis=3, tiled=True)
        reflected = complex_apply(response, gathered, 1.0)
        reflected_time = lax.all_to_all(
            reflected.astype(jnp.bfloat16), "freq", split_axis=2, concat_axis=0, tiled=True
        )
        upgoing = window * to_time(reflected_time, inverse)
        spectra_up = lax.all_to_all(
            to_spectrum(upgoing, forward), "freq", split_axis=0, concat_axis=2, tiled=True
        )
        receivers = lax.all_gather(spectra_up, "rec", axis=3, tiled=True)
        returned = complex_apply(response, receivers, -1.0)
        returned_time = lax.all_to_all(
            returned.astype(jnp.bfloat16), "freq", split_axis=2, concat_axis=0, tiled=True
        )
        coda = window * to_time(returned_time, inverse)
    return (upgoing, coda)


def solution(mesh):
    placed = (P("freq", None, "rec", None), P("rec", "freq", None), P("rec", "freq"))
    return jax.shard_map(
        body,
        mesh=mesh,
        in_specs=placed,
        out_specs=(P("rec", "freq", None), P("rec", "freq", None)),
        check_vma=False,
    )
```

profile of v0, /device:TPU:96, one launch (start us, length us, event | category | flops | bytes accessed | tf_op | source)
XLA Modules:
  0.0 545.7 jit_solution(14085154062390279766)
XLA Ops:
  7.2 0.5 fusion.96
  7.8 1.1 fusion.39
  9.1 0.4 reshape.396
  9.5 14.9 %all_to_all.144 = bf16[8,2,3584]{2,1,0:T(2,128)(2,1)S(1)} all-to-all(bf16[8,2,3584]{2,1,0:T(2,128)(2,1)S(1)} %reshape.396), channel_id=1, replica_groups=mesh['freq'=8,'rec'=32] {'freq'}, dimensions={0} | all-to-all | bytes 229376 | tf_op jit(solution)/shard_map/all_to_all | solution.py:54
  24.4 0.4 reshape.397
  24.9 1.5 copy.89
  26.4 0.6 fusion.97
  27.0 87.4 %all-gather.5.cloned.1.call-done = bf16[16,2,32,1792]{2,0,1,3:T(8,128)(2,1)} async-done(((bf16[16,2,32,56]{2,0,1,3:T(8,128)(2,1)}), bf16[16,2,32,1792]{2,0,1,3:T(8,128)(2,1)}) %all-gather.5.cloned.1.call-update) | async-done | bytes 3670032 | tf_op jit(solution)/shard_map/all_gather | solution.py:57
  114.4 15.0 %fusion.17 = f32[2,2,16,32,56]{4,3,0,1,2:T(8,128)S(1)} fusion(bf16[16,2,56,1792]{3,2,1,0:T(8,128)(2,1)} %param.3, bf16[16,2,32,1792,1]{2,0,1,3,4:T(8,128)(2,1)} %bitcast.271), kind=kOutput, calls=%fused_computation.13 | convolution fusion | flops 411041792 | bytes 10551296 | tf_op jit(solution)/shard_map/fcrs,fdvs->cdfvr/dot_general | solution.py:41
  129.7 1.1 reshape.398
  130.8 6.7 %all-to-all-start.1 = ((bf16[8,2,3584]{2,1,0:T(2,128)(2,1)}), bf16[8,2,3584]{2,1,0:T(2,128)(2,1)S(1)}, u32[]{:S(2)}, u32[]{:S(2)}) async-start(bf16[8,2,3584]{2,1,0:T(2,128)(2,1)} %reshape.398), calls=%async_computation.1 | async-start | bytes 229376 | tf_op jit(solution)/shard_map/all_to_all | solution.py:59
  137.6 8.1 %all-to-all-done.1 = bf16[8,2,3584]{2,1,0:T(2,128)(2,1)S(1)} async-done(((bf16[8,2,3584]{2,1,0:T(2,128)(2,1)}), bf16[8,2,3584]{2,1,0:T(2,128)(2,1)S(1)}, u32[]{:S(2)}, u32[]{:S(2)}) %all-to-all-start.1) | async-done | bytes 114720 | tf_op jit(solution)/shard_map/all_to_all | solution.py:59
  145.6 0.4 reshape.399
  146.1 0.4 fusion.40
  146.7 0.4 reshape.400
  147.1 10.5 %all_to_all.145 = bf16[8,2,3584]{2,1,0:T(2,128)(2,1)S(1)} all-to-all(bf16[8,2,3584]{2,1,0:T(2,128)(2,1)S(1)} %reshape.400), channel_id=1, replica_groups=mesh['freq'=8,'rec'=32] {'freq'}, dimensions={0} | all-to-all | bytes 229376 | tf_op jit(solution)/shard_map/all_to_all | solution.py:63
  157.6 0.4 reshape.401
  158.2 1.5 copy.99
  159.9 85.8 %all-gather.7.cloned.1.call-done = bf16[16,2,32,1792]{2,0,1,3:T(8,128)(2,1)} async-done(((bf16[16,2,32,56]{2,0,1,3:T(8,128)(2,1)}), bf16[16,2,32,1792]{2,0,1,3:T(8,128)(2,1)}) %all-gather.7.cloned.1.call-update) | async-done | bytes 3670032 | tf_op jit(solution)/shard_map/all_gather | solution.py:66
  245.6 15.1 %fusion.22 = f32[2,2,16,32,56]{4,3,0,1,2:T(8,128)S(1)} fusion(bf16[16,2,56,1792]{3,2,1,0:T(8,128)(2,1)} %param.3, bf16[16,2,32,1792,1]{2,0,1,3,4:T(8,128)(2,1)} %bitcast.272), kind=kOutput, calls=%fused_computation.14 | convolution fusion | flops 411041792 | bytes 10551296 | tf_op jit(solution)/shard_map/fcrs,fdvs->cdfvr/dot_general | solution.py:41
  261.0 0.4 reshape.402
  261.4 14.6 %all_to_all.146 = bf16[8,2,3584]{2,1,0:T(2,128)(2,1)S(1)} all-to-all(bf16[8,2,3584]{2,1,0:T(2,128)(2,1)S(1)} %reshape.402), channel_id=1, replica_groups=mesh['freq'=8,'rec'=32] {'freq'}, dimensions={0} | all-to-all | bytes 229376 | tf_op jit(solution)/shard_map/all_to_all | solution.py:68
  276.1 0.4 reshape.403
  276.5 0.4 fusion.41
  277.1 0.4 reshape.404
  277.5 10.5 %all_to_all.147 = bf16[8,2,3584]{2,1,0:T(2,128)(2,1)S(1)} all-to-all(bf16[8,2,3584]{2,1,0:T(2,128)(2,1)S(1)} %reshape.404), channel_id=1, replica_groups=mesh['freq'=8,'rec'=32] {'freq'}, dimensions={0} | all-to-all | bytes 229376 | tf_op jit(solution)/shard_map/all_to_all | solution.py:54
  288.1 0.4 reshape.405
  288.6 1.5 copy.111
  290.1 0.3 all-gather.11.cloned.1.call-start
  290.3 85.7 %all-gather.9.cloned.1.call-done = bf16[16,2,32,1792]{2,0,1,3:T(8,128)(2,1)} async-done(((bf16[16,2,32,56]{2,0,1,3:T(8,128)(2,1)}), bf16[16,2,32,1792]{2,0,1,3:T(8,128)(2,1)}) %all-gather.9.cloned.1.call-update) | async-done | bytes 3670032 | tf_op jit(solution)/shard_map/all_gather | solution.py:57
  376.0 15.0 %fusion.27 = f32[2,2,16,32,56]{4,3,0,1,2:T(8,128)S(1)} fusion(bf16[16,2,56,1792]{3,2,1,0:T(8,128)(2,1)} %param.3, bf16[16,2,32,1792,1]{2,0,1,3,4:T(8,128)(2,1)} %bitcast.273), kind=kOutput, calls=%fused_computation.15 | convolution fusion | flops 411041792 | bytes 10551296 | tf_op jit(solution)/shard_map/fcrs,fdvs->cdfvr/dot_general | solution.py:41
  391.3 0.4 reshape.406
  391.8 14.6 %all_to_all.148 = bf16[8,2,3584]{2,1,0:T(2,128)(2,1)S(1)} all-to-all(bf16[8,2,3584]{2,1,0:T(2,128)(2,1)S(1)} %reshape.406), channel_id=1, replica_groups=mesh['freq'=8,'rec'=32] {'freq'}, dimensions={0} | all-to-all | bytes 229376 | tf_op jit(solution)/shard_map/all_to_all | solution.py:59
  406.4 0.4 reshape.407
  406.9 0.2 fusion.37
  407.5 0.4 reshape.408
  407.9 10.5 %all_to_all.149 = bf16[8,2,3584]{2,1,0:T(2,128)(2,1)S(1)} all-to-all(bf16[8,2,3584]{2,1,0:T(2,128)(2,1)S(1)} %reshape.408), channel_id=1, replica_groups=mesh['freq'=8,'rec'=32] {'freq'}, dimensions={0} | all-to-all | bytes 229376 | tf_op jit(solution)/shard_map/all_to_all | solution.py:63
  418.5 0.4 reshape.409
  419.0 1.5 copy.121
  420.5 86.0 %all-gather.11.cloned.1.call-done = bf16[16,2,32,1792]{2,0,1,3:T(8,128)(2,1)} async-done(((bf16[16,2,32,56]{2,0,1,3:T(8,128)(2,1)}), bf16[16,2,32,1792]{2,0,1,3:T(8,128)(2,1)}) %all-gather.11.cloned.1.call-update) | async-done | bytes 3670032 | tf_op jit(solution)/shard_map/all_gather | solution.py:66
  506.5 15.0 %fusion.12 = f32[2,2,16,32,56]{4,3,2,1,0:T(8,128)S(1)} fusion(bf16[16,2,32,1792,1]{2,0,1,3,4:T(8,128)(2,1)} %bitcast.274, bf16[16,2,56,1792]{3,2,1,0:T(8,128)(2,1)} %param.3), kind=kOutput, calls=%fused_computation.12 | convolution fusion | flops 411041792 | bytes 10551296 | tf_op jit(solution)/shard_map/fcrs,fdvs->cdfvr/dot_general | solution.py:41
  521.8 1.1 reshape.410
  522.8 6.7 %all-to-all-start.7 = ((bf16[8,2,3584]{2,1,0:T(2,128)(2,1)}), bf16[8,2,3584]{2,1,0:T(2,128)(2,1)S(1)}, u32[]{:S(2)}, u32[]{:S(2)}) async-start(bf16[8,2,3584]{2,1,0:T(2,128)(2,1)} %reshape.410), calls=%async_computation.7 | async-start | bytes 229376 | tf_op jit(solution)/shard_map/all_to_all | solution.py:68
  529.5 0.8 copy.127
  530.3 7.4 %all-to-all-done.7 = bf16[8,2,3584]{2,1,0:T(2,128)(2,1)S(1)} async-done(((bf16[8,2,3584]{2,1,0:T(2,128)(2,1)}), bf16[8,2,3584]{2,1,0:T(2,128)(2,1)S(1)}, u32[]{:S(2)}, u32[]{:S(2)}) %all-to-all-start.7) | async-done | bytes 114720 | tf_op jit(solution)/shard_map/all_to_all | solution.py:68
  537.7 0.4 reshape.411
  538.2 0.2 fusion.38
  538.4 0.8 copy.128
  (45 shorter events, 2.7 us)
Async XLA Ops:
  7.2 107.3 %all-gather.5.cloned.1.call-start = ((), (), s32[]{:S(2)}) async-start(), calls=%async_computation.8 | async-start | bytes 15138816 | tf_op jit(solution)/shard_map/all_gather | solution.py:57
  114.4 31.7 %copy-start.1 = (s32[56,4]{0,1:T(4,128)S(1)}, s32[56,4]{0,1:T(4,128)}, u32[]{:S(2)}) copy-start(s32[56,4]{0,1:T(4,128)} %param.5) | copy-start | bytes 2692
  130.8 14.8 %all-to-all-start.1 = ((bf16[8,2,3584]{2,1,0:T(2,128)(2,1)}), bf16[8,2,3584]{2,1,0:T(2,128)(2,1)S(1)}, u32[]{:S(2)}, u32[]{:S(2)}) async-start(bf16[8,2,3584]{2,1,0:T(2,128)(2,1)} %reshape.398), calls=%async_computation.1 | async-start | bytes 229376 | tf_op jit(solution)/shard_map/all_to_all | solution.py:59
  137.5 108.1 %all-gather.7.cloned.1.call-start = ((), (), s32[]{:S(2)}) async-start(), calls=%async_computation.9 | async-start | bytes 15138816 | tf_op jit(solution)/shard_map/all_gather | solution.py:66
  159.6 216.4 %all-gather.9.cloned.1.call-start = ((), (), s32[]{:S(2)}) async-start(), calls=%async_computation.10 | async-start | bytes 15138816 | tf_op jit(solution)/shard_map/all_gather | solution.py:57
  245.6 30.9 %copy-start = (f32[56,4,256]{2,1,0:T(4,128)S(1)}, f32[56,4,256]{2,1,0:T(4,128)}, u32[]{:S(2)}) copy-start(f32[56,4,256]{2,1,0:T(4,128)} %param.4) | copy-start | bytes 688132
  290.1 216.4 %all-gather.11.cloned.1.call-start = ((), (), s32[]{:S(2)}) async-start(), calls=%async_computation.11 | async-start | bytes 15138816 | tf_op jit(solution)/shard_map/all_gather | solution.py:66
  522.8 14.8 %all-to-all-start.7 = ((bf16[8,2,3584]{2,1,0:T(2,128)(2,1)}), bf16[8,2,3584]{2,1,0:T(2,128)(2,1)S(1)}, u32[]{:S(2)}, u32[]{:S(2)}) async-start(bf16[8,2,3584]{2,1,0:T(2,128)(2,1)} %reshape.410), calls=%async_computation.7 | async-start | bytes 229376 | tf_op jit(solution)/shard_map/all_to_all | solution.py:68
Sparse Core Ops, SparseCore 0:
  26.5 87.8 all-gather.4
  159.8 85.8 all-gather.6
  290.2 85.8 all-gather.8
  420.6 85.8 all-gather.10
where the time goes:
time: 546 us
  waiting for transfers between devices  360 us (66%)
  blocking collectives  75.7 us (14%)
  matrix products  62.6 us (11%)
  local copies, waits for them, and re-layouts  17 us (3%)
  between operations  14.2 us (3%)
  starting transfers between devices  14 us (3%)
    all_gather x2, waiting for transfers between devices, body(): gathered = lax.all_gather(sources, 'rec', axis=3, tiled=True)  173 us
    all_gather x2, waiting for transfers between devices, body(): receivers = lax.all_gather(spectra_up, 'rec', axis=3, tiled=True)  172 us
    dot_general x4, matrix products, complex_apply(): jnp.einsum('fcrs,fdvs->cdfvr', block, spectra, preferred_element_type=jnp...  60.1 us
    all_to_all x2, blocking collectives, body(): lax.all_to_all(to_spectrum(downgoing, forward), 'freq', split_axis=0, con...  25.4 us
    all_to_all x2, blocking collectives, body(): lax.all_to_all(to_spectrum(upgoing, forward), 'freq', split_axis=0, conca...  21.1 us
    all_to_all x1, blocking collectives, body(): lax.all_to_all(reflected.astype(jnp.bfloat16), 'freq', split_axis=2, conc...  14.6 us
    all_to_all x1, blocking collectives, body(): lax.all_to_all(returned.astype(jnp.bfloat16), 'freq', split_axis=2, conca...  14.6 us
  transfers between devices with their start and end apart: 6, of which 6 were waited for; matrix products, arithmetic and copies ran while one was open for 0% of the time, Pallas kernels for 0%

commit v1 on v0

--- a/solution.py
+++ b/solution.py
@@ -51,8 +51,16 @@
     upgoing = coda
     for iteration in range(ITERS):
         downgoing = direct + coda
-        sources = lax.all_to_all(
-            to_spectrum(downgoing, forward), "freq", split_axis=0, concat_axis=2, tiled=True
+        sources = jnp.concatenate(
+            lax.all_to_all(
+                jnp.stack(
+                    jnp.split(to_spectrum(downgoing, forward), lax.axis_size("freq"), axis=0)
+                ),
+                "freq",
+                0,
+                0,
+            ),
+            axis=2,
         )
         gathered = lax.all_gather(sources, "rec", axis=3, tiled=True)
         reflected = complex_apply(response, gathered, 1.0)

time: 546 us -> 557 us (1.020); the launches traced: 546 us -> 549 us
  no operation moved by 1% of the time
where the time goes in v1:
time: 557 us; the launch traced here: 549 us
  waiting for transfers between devices  361 us (65%)
  blocking collectives  76.4 us (14%)
  matrix products  62.6 us (11%)
  local copies, waits for them, and re-layouts  18.9 us (3%)
  between operations  14.5 us (3%)
  starting transfers between devices  13.7 us (2%)
    all_gather x2, waiting for transfers between devices, body(): gathered = lax.all_gather(sources, 'rec', axis=3, tiled=True)  173 us
    all_gather x2, waiting for transfers between devices, body(): receivers = lax.all_gather(spectra_up, 'rec', axis=3, tiled=True)  172 us
    dot_general x4, matrix products, complex_apply(): jnp.einsum('fcrs,fdvs->cdfvr', block, spectra, preferred_element_type=jnp...  60.1 us
    all_to_all x2, blocking collectives, body(): lax.all_to_all(jnp.stack(jnp.split(to_spectrum(downgoing, forward), lax.a...  25.4 us
    all_to_all x2, blocking collectives, body(): lax.all_to_all(to_spectrum(upgoing, forward), 'freq', split_axis=0, conca...  21.7 us
    all_to_all x1, blocking collectives, body(): lax.all_to_all(returned.astype(jnp.bfloat16), 'freq', split_axis=2, conca...  14.6 us
    all_to_all x1, blocking collectives, body(): lax.all_to_all(reflected.astype(jnp.bfloat16), 'freq', split_axis=2, conc...  14.6 us
  transfers between devices with their start and end apart: 6, of which 6 were waited for; matrix products, arithmetic and copies ran while one was open for 0% of the time, Pallas kernels for 0%

profile of v1, /device:TPU:96, one launch (start us, length us, event | category | flops | bytes accessed | tf_op | source)
XLA Modules:
  0.0 548.6 jit_solution(10758730276400449760)
XLA Ops:
  7.2 0.5 fusion.96
  7.8 1.1 fusion.39
  8.9 0.3 slice_bitcast_fusion.14
  10.2 0.4 reshape.412
  10.6 14.9 %all_to_all.118 = bf16[8,2,3584]{2,1,0:T(2,128)(2,1)S(1)} all-to-all(bf16[8,2,3584]{2,1,0:T(2,128)(2,1)S(1)} %reshape.412), channel_id=1, replica_groups=mesh['freq'=8,'rec'=32] {'freq'}, dimensions={0} | all-to-all | bytes 229376 | tf_op jit(solution)/shard_map/all_to_all | solution.py:55
  25.4 0.4 reshape.413
  25.9 1.5 copy.109
  27.4 0.6 fusion.97
  28.0 87.4 %all-gather.5.cloned.1.call-done = bf16[16,2,32,1792]{2,0,1,3:T(8,128)(2,1)} async-done(((bf16[16,2,32,56]{2,0,1,3:T(8,128)(2,1)}), bf16[16,2,32,1792]{2,0,1,3:T(8,128)(2,1)}) %all-gather.5.cloned.1.call-update) | async-done | bytes 3670032 | tf_op jit(solution)/shard_map/all_gather | solution.py:65
  115.4 15.0 %fusion.17 = f32[2,2,16,32,56]{4,3,0,1,2:T(8,128)S(1)} fusion(bf16[16,2,56,1792]{3,2,1,0:T(8,128)(2,1)} %param.3, bf16[16,2,32,1792,1]{2,0,1,3,4:T(8,128)(2,1)} %bitcast.307), kind=kOutput, calls=%fused_computation.13 | convolution fusion | flops 411041792 | bytes 10551296 | tf_op jit(solution)/shard_map/fcrs,fdvs->cdfvr/dot_general | solution.py:41
  130.8 1.1 reshape.414
  131.8 6.7 %all-to-all-start.1 = ((bf16[8,2,3584]{2,1,0:T(2,128)(2,1)}), bf16[8,2,3584]{2,1,0:T(2,128)(2,1)S(1)}, u32[]{:S(2)}, u32[]{:S(2)}) async-start(bf16[8,2,3584]{2,1,0:T(2,128)(2,1)} %reshape.414), calls=%async_computation.1 | async-start | bytes 229376 | tf_op jit(solution)/shard_map/all_to_all | solution.py:67
  138.6 8.1 %all-to-all-done.1 = bf16[8,2,3584]{2,1,0:T(2,128)(2,1)S(1)} async-done(((bf16[8,2,3584]{2,1,0:T(2,128)(2,1)}), bf16[8,2,3584]{2,1,0:T(2,128)(2,1)S(1)}, u32[]{:S(2)}, u32[]{:S(2)}) %all-to-all-start.1) | async-done | bytes 114720 | tf_op jit(solution)/shard_map/all_to_all | solution.py:67
  146.7 0.4 reshape.415
  147.1 0.4 fusion.40
  147.7 0.4 reshape.416
  148.1 11.0 %all_to_all.119 = bf16[8,2,3584]{2,1,0:T(2,128)(2,1)S(1)} all-to-all(bf16[8,2,3584]{2,1,0:T(2,128)(2,1)S(1)} %reshape.416), channel_id=1, replica_groups=mesh['freq'=8,'rec'=32] {'freq'}, dimensions={0} | all-to-all | bytes 229376 | tf_op jit(solution)/shard_map/all_to_all | solution.py:71
  159.1 0.4 reshape.417
  159.6 1.5 copy.119
  161.2 85.9 %all-gather.7.cloned.1.call-done = bf16[16,2,32,1792]{2,0,1,3:T(8,128)(2,1)} async-done(((bf16[16,2,32,56]{2,0,1,3:T(8,128)(2,1)}), bf16[16,2,32,1792]{2,0,1,3:T(8,128)(2,1)}) %all-gather.7.cloned.1.call-update) | async-done | bytes 3670032 | tf_op jit(solution)/shard_map/all_gather | solution.py:74
  247.1 15.1 %fusion.22 = f32[2,2,16,32,56]{4,3,0,1,2:T(8,128)S(1)} fusion(bf16[16,2,56,1792]{3,2,1,0:T(8,128)(2,1)} %param.3, bf16[16,2,32,1792,1]{2,0,1,3,4:T(8,128)(2,1)} %bitcast.308), kind=kOutput, calls=%fused_computation.14 | convolution fusion | flops 411041792 | bytes 10551296 | tf_op jit(solution)/shard_map/fcrs,fdvs->cdfvr/dot_general | solution.py:41
  262.5 0.4 reshape.418
  262.9 14.6 %all_to_all.120 = bf16[8,2,3584]{2,1,0:T(2,128)(2,1)S(1)} all-to-all(bf16[8,2,3584]{2,1,0:T(2,128)(2,1)S(1)} %reshape.418), channel_id=1, replica_groups=mesh['freq'=8,'rec'=32] {'freq'}, dimensions={0} | all-to-all | bytes 229376 | tf_op jit(solution)/shard_map/all_to_all | solution.py:76
  277.5 0.4 reshape.419
  278.0 0.4 fusion.41
  278.4 0.3 slice_bitcast_fusion.6
  279.6 0.4 reshape.420
  280.0 10.5 %all_to_all.121 = bf16[8,2,3584]{2,1,0:T(2,128)(2,1)S(1)} all-to-all(bf16[8,2,3584]{2,1,0:T(2,128)(2,1)S(1)} %reshape.420), channel_id=1, replica_groups=mesh['freq'=8,'rec'=32] {'freq'}, dimensions={0} | all-to-all | bytes 229376 | tf_op jit(solution)/shard_map/all_to_all | solution.py:55
  290.5 0.4 reshape.421
  291.0 1.5 copy.137
  292.7 85.8 %all-gather.9.cloned.1.call-done = bf16[16,2,32,1792]{2,0,1,3:T(8,128)(2,1)} async-done(((bf16[16,2,32,56]{2,0,1,3:T(8,128)(2,1)}), bf16[16,2,32,1792]{2,0,1,3:T(8,128)(2,1)}) %all-gather.9.cloned.1.call-update) | async-done | bytes 3670032 | tf_op jit(solution)/shard_map/all_gather | solution.py:65
  378.5 15.0 %fusion.27 = f32[2,2,16,32,56]{4,3,0,1,2:T(8,128)S(1)} fusion(bf16[16,2,56,1792]{3,2,1,0:T(8,128)(2,1)} %param.3, bf16[16,2,32,1792,1]{2,0,1,3,4:T(8,128)(2,1)} %bitcast.309), kind=kOutput, calls=%fused_computation.15 | convolution fusion | flops 411041792 | bytes 10551296 | tf_op jit(solution)/shard_map/fcrs,fdvs->cdfvr/dot_general | solution.py:41
  393.8 0.4 reshape.422
  394.2 14.6 %all_to_all.122 = bf16[8,2,3584]{2,1,0:T(2,128)(2,1)S(1)} all-to-all(bf16[8,2,3584]{2,1,0:T(2,128)(2,1)S(1)} %reshape.422), channel_id=1, replica_groups=mesh['freq'=8,'rec'=32] {'freq'}, dimensions={0} | all-to-all | bytes 229376 | tf_op jit(solution)/shard_map/all_to_all | solution.py:67
  408.9 0.4 reshape.423
  409.3 0.2 fusion.37
  410.0 0.4 reshape.424
  410.4 10.7 %all_to_all.123 = bf16[8,2,3584]{2,1,0:T(2,128)(2,1)S(1)} all-to-all(bf16[8,2,3584]{2,1,0:T(2,128)(2,1)S(1)} %reshape.424), channel_id=1, replica_groups=mesh['freq'=8,'rec'=32] {'freq'}, dimensions={0} | all-to-all | bytes 229376 | tf_op jit(solution)/shard_map/all_to_all | solution.py:71
  421.1 0.4 reshape.425
  421.6 1.5 copy.147
  423.1 86.0 %all-gather.11.cloned.1.call-done = bf16[16,2,32,1792]{2,0,1,3:T(8,128)(2,1)} async-done(((bf16[16,2,32,56]{2,0,1,3:T(8,128)(2,1)}), bf16[16,2,32,1792]{2,0,1,3:T(8,128)(2,1)}) %all-gather.11.cloned.1.call-update) | async-done | bytes 3670032 | tf_op jit(solution)/shard_map/all_gather | solution.py:74
  509.1 15.0 %fusion.12 = f32[2,2,16,32,56]{4,3,2,1,0:T(8,128)S(1)} fusion(bf16[16,2,32,1792,1]{2,0,1,3,4:T(8,128)(2,1)} %bitcast.310, bf16[16,2,56,1792]{3,2,1,0:T(8,128)(2,1)} %param.3), kind=kOutput, calls=%fused_computation.12 | convolution fusion | flops 411041792 | bytes 10551296 | tf_op jit(solution)/shard_map/fcrs,fdvs->cdfvr/dot_general | solution.py:41
  524.4 1.1 reshape.426
  525.5 6.7 %all-to-all-start.7 = ((bf16[8,2,3584]{2,1,0:T(2,128)(2,1)}), bf16[8,2,3584]{2,1,0:T(2,128)(2,1)S(1)}, u32[]{:S(2)}, u32[]{:S(2)}) async-start(bf16[8,2,3584]{2,1,0:T(2,128)(2,1)} %reshape.426), calls=%async_computation.7 | async-start | bytes 229376 | tf_op jit(solution)/shard_map/all_to_all | solution.py:76
  532.2 0.8 copy.153
  533.0 7.4 %all-to-all-done.7 = bf16[8,2,3584]{2,1,0:T(2,128)(2,1)S(1)} async-done(((bf16[8,2,3584]{2,1,0:T(2,128)(2,1)}), bf16[8,2,3584]{2,1,0:T(2,128)(2,1)S(1)}, u32[]{:S(2)}, u32[]{:S(2)}) %all-to-all-start.7) | async-done | bytes 114720 | tf_op jit(solution)/shard_map/all_to_all | solution.py:76
  540.3 0.4 reshape.427
  541.0 0.8 copy.154
  (75 shorter events, 4.3 us)
Async XLA Ops:
  7.2 108.3 %all-gather.5.cloned.1.call-start = ((), (), s32[]{:S(2)}) async-start(), calls=%async_computation.8 | async-start | bytes 15138816 | tf_op jit(solution)/shard_map/all_gather | solution.py:65
  115.4 31.7 %copy-start.1 = (s32[56,4]{0,1:T(4,128)S(1)}, s32[56,4]{0,1:T(4,128)}, u32[]{:S(2)}) copy-start(s32[56,4]{0,1:T(4,128)} %param.5) | copy-start | bytes 2692
  131.8 14.8 %all-to-all-start.1 = ((bf16[8,2,3584]{2,1,0:T(2,128)(2,1)}), bf16[8,2,3584]{2,1,0:T(2,128)(2,1)S(1)}, u32[]{:S(2)}, u32[]{:S(2)}) async-start(bf16[8,2,3584]{2,1,0:T(2,128)(2,1)} %reshape.414), calls=%async_computation.1 | async-start | bytes 229376 | tf_op jit(solution)/shard_map/all_to_all | solution.py:67
  138.5 108.6 %all-gather.7.cloned.1.call-start = ((), (), s32[]{:S(2)}) async-start(), calls=%async_computation.9 | async-start | bytes 15138816 | tf_op jit(solution)/shard_map/all_gather | solution.py:74
  161.1 217.4 %all-gather.9.cloned.1.call-start = ((), (), s32[]{:S(2)}) async-start(), calls=%async_computation.10 | async-start | bytes 15138816 | tf_op jit(solution)/shard_map/all_gather | solution.py:65
  247.1 30.9 %copy-start = (f32[56,4,256]{2,1,0:T(4,128)S(1)}, f32[56,4,256]{2,1,0:T(4,128)}, u32[]{:S(2)}) copy-start(f32[56,4,256]{2,1,0:T(4,128)} %param.4) | copy-start | bytes 688132
  292.5 216.6 %all-gather.11.cloned.1.call-start = ((), (), s32[]{:S(2)}) async-start(), calls=%async_computation.11 | async-start | bytes 15138816 | tf_op jit(solution)/shard_map/all_gather | solution.py:74
  525.5 14.8 %all-to-all-start.7 = ((bf16[8,2,3584]{2,1,0:T(2,128)(2,1)}), bf16[8,2,3584]{2,1,0:T(2,128)(2,1)S(1)}, u32[]{:S(2)}, u32[]{:S(2)}) async-start(bf16[8,2,3584]{2,1,0:T(2,128)(2,1)} %reshape.426), calls=%async_computation.7 | async-start | bytes 229376 | tf_op jit(solution)/shard_map/all_to_all | solution.py:76
Sparse Core Ops, SparseCore 0:
  27.5 87.8 all-gather.4
  161.2 85.8 all-gather.6
  292.6 85.8 all-gather.8
  423.2 85.8 all-gather.10
